TPU v7x, 8 devices: a whole 2x2x1 slice. The times are simulated.
8 devices in a mesh: parts: 1 (over z), col: 2 (over y), row: 2 (over x), sub: 2 (over core).
Axes of the slice: x: 2, y: 2, z: 1, core: 2. Of those that a mesh axis runs over, the one named last changes fastest.
Arguments:
- edge_dist: float32 [16, 128, 2048], P(('parts', 'row', 'sub'), None, 'col')
Outputs:
- output: float32 [16, 128, 2048], P(('parts', 'row', 'sub'), None, 'col')
All inputs are finite; a program needn't handle non-finite values.
Results may differ from a plain program's by a relative error of at most 0.001.
Values sent between devices are 32-bit elements.
A program may use at most 1 GiB of HBM per device.

v0:
```python
import jax
import jax.numpy as jnp
from jax import lax
from jax.sharding import PartitionSpec as P


def close_block(block_in):
    last_axis = block_in.ndim - 1
    def pivot_step(pivot_idx, current):
        col_vec = lax.dynamic_slice_in_dim(current, pivot_idx, 1, axis=last_axis)
        row_vec = lax.dynamic_slice_in_dim(current, pivot_idx, 1, axis=last_axis - 1)
        return jnp.minimum(current, col_vec + row_vec)
    return lax.fori_loop(0, block_in.shape[-1], pivot_step, block_in)


def min_plus(left_mat, right_mat):
    return jnp.min(jnp.expand_dims(left_mat, -1) + jnp.expand_dims(right_mat, -3), axis=-2)


def solution(mesh):
    row_devs = mesh.shape['row'] * mesh.shape['sub']
    col_devs = mesh.shape['col']
    sub_devs = mesh.shape['sub']
    dist_spec = P(('parts', 'row', 'sub'), None, 'col')

    def local_run(local_dist):
        rows_local, blk_size, cols_width = local_dist.shape
        rounds = rows_local * row_devs
        my_row = lax.axis_index('row') * sub_devs + lax.axis_index('sub')
        my_col = lax.axis_index('col')
        current = local_dist
        for round_idx in range(rounds):
            in_row = my_row == round_idx % row_devs
            in_col = my_col == round_idx % col_devs
            row_pos = round_idx // row_devs
            col_pos = (round_idx // col_devs) * blk_size
            diag_blk = close_block(current[row_pos, :, col_pos:col_pos + blk_size])
            diag_blk = lax.pmin(jnp.where(in_row & in_col, diag_blk, jnp.inf), ('row', 'sub', 'col'))
            row_pan = min_plus(diag_blk, current[row_pos])
            row_pan = lax.pmin(jnp.where(in_row, row_pan, jnp.inf), ('row', 'sub'))
            col_pan = min_plus(current[:, :, col_pos:col_pos + blk_size], diag_blk)
            col_pan = lax.pmin(jnp.where(in_col, col_pan, jnp.inf), 'col')
            current = jnp.minimum(current, min_plus(col_pan, row_pan))
        return current

    return jax.shard_map(local_run, mesh=mesh, in_specs=(dist_spec,), out_specs=dist_spec, check_vma=False)
```

profile of v0, /device:TPU:7, one launch (start us, length us, event | category | flops | bytes accessed | tf_op | source)
XLA Modules:
  0.0 3585.7 jit_solution(8144983994606697279)
XLA Ops:
  47.8 39.6 %all-reduce.49.cloned.1.call-done = f32[128,128]{1,0:T(8,128)} async-done(((f32[128,128]{1,0:T(8,128)}), f32[128,128]{1,0:T(8,128)}) %all-reduce.49.cloned.1.call-update) | async-done | bytes 65552 | tf_op jit(solution)/shard_map/pmin | solution.py:38
  148.3 79.8 %add_reduce_fusion.15 = f32[4,128,1024]{2,1,0:T(8,128)S(1)} fusion(f32[128,1024]{1,0:T(8,128)} %all-reduce.53.cloned.1.call-done, f32[4,128,128]{2,1,0:T(8,128)} %all-reduce.51.cloned.1.call-done), kind=kLoop, calls=%fused_computation.79 | loop fusion | flops 133693440 | bytes 2883584 | tf_op jit(solution)/shard_map/reduce_min | solution.py:17
  269.6 41.3 %all-reduce.55.cloned.1.call-done = f32[128,128]{1,0:T(8,128)} async-done(((f32[128,128]{1,0:T(8,128)}), f32[128,128]{1,0:T(8,128)}) %all-reduce.55.cloned.1.call-update) | async-done | bytes 65552 | tf_op jit(solution)/shard_map/pmin | solution.py:38
  371.7 79.8 %add_reduce_fusion.14 = f32[4,128,1024]{2,1,0:T(8,128)S(1)} fusion(f32[128,1024]{1,0:T(8,128)} %all-reduce.59.cloned.1.call-done, f32[4,128,128]{2,1,0:T(8,128)} %all-reduce.57.cloned.1.call-done), kind=kLoop, calls=%fused_computation.78 | loop fusion | flops 133693440 | bytes 2883584 | tf_op jit(solution)/shard_map/reduce_min | solution.py:17
  493.0 41.3 %all-reduce.61.cloned.1.call-done = f32[128,128]{1,0:T(8,128)} async-done(((f32[128,128]{1,0:T(8,128)}), f32[128,128]{1,0:T(8,128)}) %all-reduce.61.cloned.1.call-update) | async-done | bytes 65552 | tf_op jit(solution)/shard_map/pmin | solution.py:38
  595.1 79.8 %add_reduce_fusion.13 = f32[4,128,1024]{2,1,0:T(8,128)S(1)} fusion(f32[128,1024]{1,0:T(8,128)} %all-reduce.65.cloned.1.call-done, f32[4,128,128]{2,1,0:T(8,128)} %all-reduce.63.cloned.1.call-done), kind=kLoop, calls=%fused_computation.77 | loop fusion | flops 133693440 | bytes 2883584 | tf_op jit(solution)/shard_map/reduce_min | solution.py:17
  717.1 40.3 %all-reduce.67.cloned.1.call-done = f32[128,128]{1,0:T(8,128)} async-done(((f32[128,128]{1,0:T(8,128)}), f32[128,128]{1,0:T(8,128)}) %all-reduce.67.cloned.1.call-update) | async-done | bytes 65552 | tf_op jit(solution)/shard_map/pmin | solution.py:38
  818.3 79.8 %add_reduce_fusion.12 = f32[4,128,1024]{2,1,0:T(8,128)S(1)} fusion(f32[128,1024]{1,0:T(8,128)} %all-reduce.71.cloned.1.call-done, f32[4,128,128]{2,1,0:T(8,128)} %all-reduce.69.cloned.1.call-done), kind=kLoop, calls=%fused_computation.76 | loop fusion | flops 133693440 | bytes 2883584 | tf_op jit(solution)/shard_map/reduce_min | solution.py:17
  940.3 40.3 %all-reduce.73.cloned.1.call-done = f32[128,128]{1,0:T(8,128)} async-done(((f32[128,128]{1,0:T(8,128)}), f32[128,128]{1,0:T(8,128)}) %all-reduce.73.cloned.1.call-update) | async-done | bytes 65552 | tf_op jit(solution)/shard_map/pmin | solution.py:38
  1041.5 79.8 %add_reduce_fusion.11 = f32[4,128,1024]{2,1,0:T(8,128)S(1)} fusion(f32[128,1024]{1,0:T(8,128)} %all-reduce.77.cloned.1.call-done, f32[4,128,128]{2,1,0:T(8,128)} %all-reduce.75.cloned.1.call-done), kind=kLoop, calls=%fused_computation.75 | loop fusion | flops 133693440 | bytes 2883584 | tf_op jit(solution)/shard_map/reduce_min | solution.py:17
  1163.4 40.3 %all-reduce.79.cloned.1.call-done = f32[128,128]{1,0:T(8,128)} async-done(((f32[128,128]{1,0:T(8,128)}), f32[128,128]{1,0:T(8,128)}) %all-reduce.79.cloned.1.call-update) | async-done | bytes 65552 | tf_op jit(solution)/shard_map/pmin | solution.py:38
  1265.0 79.8 %add_reduce_fusion.10 = f32[4,128,1024]{2,1,0:T(8,128)S(1)} fusion(f32[128,1024]{1,0:T(8,128)} %all-reduce.83.cloned.1.call-done, f32[4,128,128]{2,1,0:T(8,128)} %all-reduce.81.cloned.1.call-done), kind=kLoop, calls=%fused_computation.74 | loop fusion | flops 133693440 | bytes 2883584 | tf_op jit(solution)/shard_map/reduce_min | solution.py:17
  1387.0 40.3 %all-reduce.85.cloned.1.call-done = f32[128,128]{1,0:T(8,128)} async-done(((f32[128,128]{1,0:T(8,128)}), f32[128,128]{1,0:T(8,128)}) %all-reduce.85.cloned.1.call-update) | async-done | bytes 65552 | tf_op jit(solution)/shard_map/pmin | solution.py:38
  1488.2 79.8 %add_reduce_fusion.9 = f32[4,128,1024]{2,1,0:T(8,128)S(1)} fusion(f32[128,1024]{1,0:T(8,128)} %all-reduce.89.cloned.1.call-done, f32[4,128,128]{2,1,0:T(8,128)} %all-reduce.87.cloned.1.call-done), kind=kLoop, calls=%fused_computation.73 | loop fusion | flops 133693440 | bytes 2883584 | tf_op jit(solution)/shard_map/reduce_min | solution.py:17
  1610.2 40.3 %all-reduce.91.cloned.1.call-done = f32[128,128]{1,0:T(8,128)} async-done(((f32[128,128]{1,0:T(8,128)}), f32[128,128]{1,0:T(8,128)}) %all-reduce.91.cloned.1.call-update) | async-done | bytes 65552 | tf_op jit(solution)/shard_map/pmin | solution.py:38
  1711.4 79.8 %add_reduce_fusion.8 = f32[4,128,1024]{2,1,0:T(8,128)S(1)} fusion(f32[128,1024]{1,0:T(8,128)} %all-reduce.95.cloned.1.call-done, f32[4,128,128]{2,1,0:T(8,128)} %all-reduce.93.cloned.1.call-done), kind=kLoop, calls=%fused_computation.72 | loop fusion | flops 133693440 | bytes 2883584 | tf_op jit(solution)/shard_map/reduce_min | solution.py:17
  1833.5 40.1 %all-reduce.97.cloned.1.call-done = f32[128,128]{1,0:T(8,128)} async-done(((f32[128,128]{1,0:T(8,128)}), f32[128,128]{1,0:T(8,128)}) %all-reduce.97.cloned.1.call-update) | async-done | bytes 65552 | tf_op jit(solution)/shard_map/pmin | solution.py:38
  1934.6 79.8 %add_reduce_fusion.7 = f32[4,128,1024]{2,1,0:T(8,128)S(1)} fusion(f32[128,1024]{1,0:T(8,128)} %all-reduce.101.cloned.1.call-done, f32[4,128,128]{2,1,0:T(8,128)} %all-reduce.99.cloned.1.call-done), kind=kLoop, calls=%fused_computation.71 | loop fusion | flops 133693440 | bytes 2883584 | tf_op jit(solution)/shard_map/reduce_min | solution.py:17
  2056.5 40.3 %all-reduce.103.cloned.1.call-done = f32[128,128]{1,0:T(8,128)} async-done(((f32[128,128]{1,0:T(8,128)}), f32[128,128]{1,0:T(8,128)}) %all-reduce.103.cloned.1.call-update) | async-done | bytes 65552 | tf_op jit(solution)/shard_map/pmin | solution.py:38
  2157.7 79.8 %add_reduce_fusion.6 = f32[4,128,1024]{2,1,0:T(8,128)S(1)} fusion(f32[128,1024]{1,0:T(8,128)} %all-reduce.107.cloned.1.call-done, f32[4,128,128]{2,1,0:T(8,128)} %all-reduce.105.cloned.1.call-done), kind=kLoop, calls=%fused_computation.70 | loop fusion | flops 133693440 | bytes 2883584 | tf_op jit(solution)/shard_map/reduce_min | solution.py:17
  2279.7 40.3 %all-reduce.109.cloned.1.call-done = f32[128,128]{1,0:T(8,128)} async-done(((f32[128,128]{1,0:T(8,128)}), f32[128,128]{1,0:T(8,128)}) %all-reduce.109.cloned.1.call-update) | async-done | bytes 65552 | tf_op jit(solution)/shard_map/pmin | solution.py:38
  2380.9 79.8 %add_reduce_fusion.5 = f32[4,128,1024]{2,1,0:T(8,128)S(1)} fusion(f32[128,1024]{1,0:T(8,128)} %all-reduce.113.cloned.1.call-done, f32[4,128,128]{2,1,0:T(8,128)} %all-reduce.111.cloned.1.call-done), kind=kLoop, calls=%fused_computation.69 | loop fusion | flops 133693440 | bytes 2883584 | tf_op jit(solution)/shard_map/reduce_min | solution.py:17
  2502.9 40.3 %all-reduce.115.cloned.1.call-done = f32[128,128]{1,0:T(8,128)} async-done(((f32[128,128]{1,0:T(8,128)}), f32[128,128]{1,0:T(8,128)}) %all-reduce.115.cloned.1.call-update) | async-done | bytes 65552 | tf_op jit(solution)/shard_map/pmin | solution.py:38
  2604.1 79.8 %add_reduce_fusion.4 = f32[4,128,1024]{2,1,0:T(8,128)S(1)} fusion(f32[128,1024]{1,0:T(8,128)} %all-reduce.119.cloned.1.call-done, f32[4,128,128]{2,1,0:T(8,128)} %all-reduce.117.cloned.1.call-done), kind=kLoop, calls=%fused_computation.68 | loop fusion | flops 133693440 | bytes 2883584 | tf_op jit(solution)/shard_map/reduce_min | solution.py:17
  2725.3 41.3 %all-reduce.121.cloned.1.call-done = f32[128,128]{1,0:T(8,128)} async-done(((f32[128,128]{1,0:T(8,128)}), f32[128,128]{1,0:T(8,128)}) %all-reduce.121.cloned.1.call-update) | async-done | bytes 65552 | tf_op jit(solution)/shard_map/pmin | solution.py:38
  2827.5 79.8 %add_reduce_fusion.3 = f32[4,128,1024]{2,1,0:T(8,128)S(1)} fusion(f32[128,1024]{1,0:T(8,128)} %all-reduce.125.cloned.1.call-done, f32[4,128,128]{2,1,0:T(8,128)} %all-reduce.123.cloned.1.call-done), kind=kLoop, calls=%fused_computation.67 | loop fusion | flops 133693440 | bytes 2883584 | tf_op jit(solution)/shard_map/reduce_min | solution.py:17
  2949.4 40.3 %all-reduce.127.cloned.1.call-done = f32[128,128]{1,0:T(8,128)} async-done(((f32[128,128]{1,0:T(8,128)}), f32[128,128]{1,0:T(8,128)}) %all-reduce.127.cloned.1.call-update) | async-done | bytes 65552 | tf_op jit(solution)/shard_map/pmin | solution.py:38
  3050.9 79.8 %add_reduce_fusion.2 = f32[4,128,1024]{2,1,0:T(8,128)S(1)} fusion(f32[128,1024]{1,0:T(8,128)} %all-reduce.131.cloned.1.call-done, f32[4,128,128]{2,1,0:T(8,128)} %all-reduce.129.cloned.1.call-done), kind=kLoop, calls=%fused_computation.66 | loop fusion | flops 133693440 | bytes 2883584 | tf_op jit(solution)/shard_map/reduce_min | solution.py:17
  3172.8 40.3 %all-reduce.133.cloned.1.call-done = f32[128,128]{1,0:T(8,128)} async-done(((f32[128,128]{1,0:T(8,128)}), f32[128,128]{1,0:T(8,128)}) %all-reduce.133.cloned.1.call-update) | async-done | bytes 65552 | tf_op jit(solution)/shard_map/pmin | solution.py:38
  3274.0 79.8 %add_reduce_fusion.1 = f32[4,128,1024]{2,1,0:T(8,128)S(1)} fusion(f32[128,1024]{1,0:T(8,128)} %all-reduce.137.cloned.1.call-done, f32[4,128,128]{2,1,0:T(8,128)} %all-reduce.135.cloned.1.call-done), kind=kLoop, calls=%fused_computation.65 | loop fusion | flops 133693440 | bytes 2883584 | tf_op jit(solution)/shard_map/reduce_min | solution.py:17
  3396.0 40.3 %all-reduce.139.cloned.1.call-done = f32[128,128]{1,0:T(8,128)} async-done(((f32[128,128]{1,0:T(8,128)}), f32[128,128]{1,0:T(8,128)}) %all-reduce.139.cloned.1.call-update) | async-done | bytes 65552 | tf_op jit(solution)/shard_map/pmin | solution.py:38
  3497.2 79.8 %add_reduce_fusion = f32[4,128,1024]{2,1,0:T(8,128)S(1)} fusion(f32[128,1024]{1,0:T(8,128)} %all-reduce.143.cloned.1.call-done, f32[4,128,128]{2,1,0:T(8,128)} %all-reduce.141.cloned.1.call-done), kind=kLoop, calls=%fused_computation.64 | loop fusion | flops 133693440 | bytes 2883584 | tf_op jit(solution)/shard_map/reduce_min | solution.py:17
  (6493 shorter events, 2192.6 us)
Async XLA Ops:
  6.5 80.9 %all-reduce.49.cloned.1.call-start = ((), (), s32[]{:S(2)}) async-start(), calls=%async_computation | async-start | bytes 131072 | tf_op jit(solution)/shard_map/pmin | solution.py:38
  46.7 73.6 %all-reduce.51.cloned.1.call-start = ((), (), s32[]{:S(2)}) async-start(), calls=%async_computation.1 | async-start | bytes 524288 | tf_op jit(solution)/shard_map/pmin | solution.py:42
  120.3 190.6 %all-reduce.55.cloned.1.call-start = ((), (), s32[]{:S(2)}) async-start(), calls=%async_computation.3 | async-start | bytes 131072 | tf_op jit(solution)/shard_map/pmin | solution.py:38
  269.4 74.4 %all-reduce.57.cloned.1.call-start = ((), (), s32[]{:S(2)}) async-start(), calls=%async_computation.4 | async-start | bytes 524288 | tf_op jit(solution)/shard_map/pmin | solution.py:42
  343.7 190.6 %all-reduce.61.cloned.1.call-start = ((), (), s32[]{:S(2)}) async-start(), calls=%async_computation.6 | async-start | bytes 131072 | tf_op jit(solution)/shard_map/pmin | solution.py:38
  492.8 74.6 %all-reduce.63.cloned.1.call-start = ((), (), s32[]{:S(2)}) async-start(), calls=%async_computation.7 | async-start | bytes 524288 | tf_op jit(solution)/shard_map/pmin | solution.py:42
  567.1 190.3 %all-reduce.67.cloned.1.call-start = ((), (), s32[]{:S(2)}) async-start(), calls=%async_computation.9 | async-start | bytes 131072 | tf_op jit(solution)/shard_map/pmin | solution.py:38
  716.0 74.4 %all-reduce.69.cloned.1.call-start = ((), (), s32[]{:S(2)}) async-start(), calls=%async_computation.10 | async-start | bytes 524288 | tf_op jit(solution)/shard_map/pmin | solution.py:42
  790.3 190.3 %all-reduce.73.cloned.1.call-start = ((), (), s32[]{:S(2)}) async-start(), calls=%async_computation.12 | async-start | bytes 131072 | tf_op jit(solution)/shard_map/pmin | solution.py:38
  939.1 74.4 %all-reduce.75.cloned.1.call-start = ((), (), s32[]{:S(2)}) async-start(), calls=%async_computation.13 | async-start | bytes 524288 | tf_op jit(solution)/shard_map/pmin | solution.py:42
  1013.4 190.3 %all-reduce.79.cloned.1.call-start = ((), (), s32[]{:S(2)}) async-start(), calls=%async_computation.15 | async-start | bytes 131072 | tf_op jit(solution)/shard_map/pmin | solution.py:38
  1162.3 74.8 %all-reduce.81.cloned.1.call-start = ((), (), s32[]{:S(2)}) async-start(), calls=%async_computation.16 | async-start | bytes 524288 | tf_op jit(solution)/shard_map/pmin | solution.py:42
  1237.0 190.3 %all-reduce.85.cloned.1.call-start = ((), (), s32[]{:S(2)}) async-start(), calls=%async_computation.18 | async-start | bytes 131072 | tf_op jit(solution)/shard_map/pmin | solution.py:38
  1385.9 74.4 %all-reduce.87.cloned.1.call-start = ((), (), s32[]{:S(2)}) async-start(), calls=%async_computation.19 | async-start | bytes 524288 | tf_op jit(solution)/shard_map/pmin | solution.py:42
  1460.2 190.3 %all-reduce.91.cloned.1.call-start = ((), (), s32[]{:S(2)}) async-start(), calls=%async_computation.21 | async-start | bytes 131072 | tf_op jit(solution)/shard_map/pmin | solution.py:38
  1609.1 74.4 %all-reduce.93.cloned.1.call-start = ((), (), s32[]{:S(2)}) async-start(), calls=%async_computation.22 | async-start | bytes 524288 | tf_op jit(solution)/shard_map/pmin | solution.py:42
  1683.4 190.3 %all-reduce.97.cloned.1.call-start = ((), (), s32[]{:S(2)}) async-start(), calls=%async_computation.24 | async-start | bytes 131072 | tf_op jit(solution)/shard_map/pmin | solution.py:38
  1832.2 74.4 %all-reduce.99.cloned.1.call-start = ((), (), s32[]{:S(2)}) async-start(), calls=%async_computation.25 | async-start | bytes 524288 | tf_op jit(solution)/shard_map/pmin | solution.py:42
  1906.5 190.3 %all-reduce.103.cloned.1.call-start = ((), (), s32[]{:S(2)}) async-start(), calls=%async_computation.27 | async-start | bytes 131072 | tf_op jit(solution)/shard_map/pmin | solution.py:38
  2055.4 74.4 %all-reduce.105.cloned.1.call-start = ((), (), s32[]{:S(2)}) async-start(), calls=%async_computation.28 | async-start | bytes 524288 | tf_op jit(solution)/shard_map/pmin | solution.py:42
  2129.7 190.3 %all-reduce.109.cloned.1.call-start = ((), (), s32[]{:S(2)}) async-start(), calls=%async_computation.30 | async-start | bytes 131072 | tf_op jit(solution)/shard_map/pmin | solution.py:38
  2278.6 74.6 %all-reduce.111.cloned.1.call-start = ((), (), s32[]{:S(2)}) async-start(), calls=%async_computation.31 | async-start | bytes 524288 | tf_op jit(solution)/shard_map/pmin | solution.py:42
  2352.9 190.3 %all-reduce.115.cloned.1.call-start = ((), (), s32[]{:S(2)}) async-start(), calls=%async_computation.33 | async-start | bytes 131072 | tf_op jit(solution)/shard_map/pmin | solution.py:38
  2501.7 74.4 %all-reduce.117.cloned.1.call-start = ((), (), s32[]{:S(2)}) async-start(), calls=%async_computation.34 | async-start | bytes 524288 | tf_op jit(solution)/shard_map/pmin | solution.py:42
  2576.0 190.6 %all-reduce.121.cloned.1.call-start = ((), (), s32[]{:S(2)}) async-start(), calls=%async_computation.36 | async-start | bytes 131072 | tf_op jit(solution)/shard_map/pmin | solution.py:38
  2725.2 74.3 %all-reduce.123.cloned.1.call-start = ((), (), s32[]{:S(2)}) async-start(), calls=%async_computation.37 | async-start | bytes 524288 | tf_op jit(solution)/shard_map/pmin | solution.py:42
  2799.4 190.3 %all-reduce.127.cloned.1.call-start = ((), (), s32[]{:S(2)}) async-start(), calls=%async_computation.39 | async-start | bytes 131072 | tf_op jit(solution)/shard_map/pmin | solution.py:38
  2948.3 74.6 %all-reduce.129.cloned.1.call-start = ((), (), s32[]{:S(2)}) async-start(), calls=%async_computation.40 | async-start | bytes 524288 | tf_op jit(solution)/shard_map/pmin | solution.py:42
  3022.8 190.3 %all-reduce.133.cloned.1.call-start = ((), (), s32[]{:S(2)}) async-start(), calls=%async_computation.42 | async-start | bytes 131072 | tf_op jit(solution)/shard_map/pmin | solution.py:38
  3171.7 74.4 %all-reduce.135.cloned.1.call-start = ((), (), s32[]{:S(2)}) async-start(), calls=%async_computation.43 | async-start | bytes 524288 | tf_op jit(solution)/shard_map/pmin | solution.py:42
  3246.0 190.3 %all-reduce.139.cloned.1.call-start = ((), (), s32[]{:S(2)}) async-start(), calls=%async_computation.45 | async-start | bytes 131072 | tf_op jit(solution)/shard_map/pmin | solution.py:38
  3394.9 74.3 %all-reduce.141.cloned.1.call-start = ((), (), s32[]{:S(2)}) async-start(), calls=%async_computation.46 | async-start | bytes 524288 | tf_op jit(solution)/shard_map/pmin | solution.py:42
  (53 other events, 3142.1 us)
Sparse Core Ops, SparseCore 0:
  46.8 40.5 all-reduce.48
  120.4 27.8 all-reduce.52
  269.5 41.2 all-reduce.54
  343.8 27.8 all-reduce.58
  493.0 41.2 all-reduce.60
  567.2 27.8 all-reduce.64
  716.1 41.2 all-reduce.66
  790.4 27.8 all-reduce.70
  939.3 41.2 all-reduce.72
  1013.6 27.8 all-reduce.76
  1162.4 41.2 all-reduce.78
  1237.1 27.8 all-reduce.82
  1386.0 41.2 all-reduce.84
  1460.3 27.8 all-reduce.88
  1609.2 41.2 all-reduce.90
  1683.5 27.8 all-reduce.94
  1832.3 41.2 all-reduce.96
  1906.7 27.8 all-reduce.100
  2055.5 41.2 all-reduce.102
  2129.8 27.8 all-reduce.106
  2278.7 41.2 all-reduce.108
  2353.0 27.8 all-reduce.112
  2501.9 41.2 all-reduce.114
  2576.2 27.8 all-reduce.118
  2725.3 41.2 all-reduce.120
  2799.6 27.8 all-reduce.124
  2948.4 41.2 all-reduce.126
  3023.0 27.8 all-reduce.130
  3171.8 41.2 all-reduce.132
  3246.1 27.8 all-reduce.136
  3395.0 41.2 all-reduce.138
  3469.3 27.8 all-reduce.142
  (16 shorter events, 285.6 us)
where the time goes:
time: 3600 us; the launch traced here: 3590 us
  other arithmetic  1990 us (55%)
  waiting for transfers between devices  1100 us (31%)
  local copies, waits for them, and re-layouts  410 us (11%)
  loops' own time  71.1 us (2%)
    reduce_min x48, other arithmetic, min_plus(): jnp.min(jnp.expand_dims(left_mat, -1) + jnp.expand_dims(right_mat, -3), a...  1780 us
    pmin x16, waiting for transfers between devices, local_run(): lax.pmin(jnp.where(in_row & in_col, diag_blk, jnp.inf), ('row', 'sub', 'c...  647 us
    pmin x16, waiting for transfers between devices, local_run(): row_pan = lax.pmin(jnp.where(in_row, row_pan, jnp.inf), ('row', 'sub'))  447 us
    dynamic_slice x2048, local copies, waits for them, and re-layouts, pivot_step(): col_vec = lax.dynamic_slice_in_dim(current, pivot_idx, 1, axis=last_axis)  354 us
    min x2048, other arithmetic, pivot_step(): return jnp.minimum(current, col_vec + row_vec)  168 us

commit v1 on v0

v1 whole, which is shorter than its diff:
```python
import functools

import jax
import jax.numpy as jnp
from jax import lax
from jax.experimental import pallas as pl
from jax.experimental.pallas import tpu as pltpu
from jax.sharding import PartitionSpec as P

MESH = pl.DeviceIdType.MESH
CHUNK = 16
GROUP = 8


def close_block(src, dst, spread):
    size = src.shape[0]
    tiles_n = size // GROUP
    tile_of = lambda x: jnp.broadcast_to(x, (GROUP, size))
    tiles = [src[GROUP * i:GROUP * (i + 1), :] for i in range(tiles_n)]
    for g in range(tiles_n):
        column = lambda i, b: tile_of(tiles[i][:, GROUP * g + b:GROUP * g + b + 1])
        own = [column(g, b) for b in range(GROUP)]
        for b in range(GROUP):
            spread[b] = own[b]
        spread[GROUP] = tiles[g]
        rows = [tile_of(spread[GROUP, b:b + 1, :]) for b in range(GROUP)]
        entry = [[tile_of(spread[b, a:a + 1, :]) for b in range(GROUP)] for a in range(GROUP)]
        for m in range(GROUP):
            for a in range(GROUP):
                if a == m:
                    continue
                rows[a] = jnp.minimum(rows[a], entry[a][m] + rows[m])
                for b in range(m + 1, GROUP):
                    if a != b:
                        entry[a][b] = jnp.minimum(entry[a][b], entry[a][m] + entry[m][b])
        for i in [(g + 1 + n) % tiles_n for n in range(tiles_n)]:
            cols = own if i == g else [column(i, b) for b in range(GROUP)]
            for b in range(GROUP):
                tiles[i] = jnp.minimum(tiles[i], cols[b] + rows[b])
    for i in range(tiles_n):
        dst[GROUP * i:GROUP * (i + 1), :] = tiles[i]


def min_plus_rows(left, right, init, out):
    left_rows = left[...]
    acc = init[...]
    for l in range(left.shape[1]):
        acc = jnp.minimum(acc, left_rows[:, l:l + 1][None] + right[:, l:l + 1, :])
    out[...] = acc


def kernel(rounds, row_devs, sub_devs, x_hbm, o_hbm, cur, row_pan, col_pan, diag, spread,
           in_sem, out_sem, row_send, row_recv, relay_send, col_send, col_recv, diag_send, diag_recv):
    col_blks, row_blks, blk, _ = cur.shape
    chunks = blk // CHUNK
    half = blk // sub_devs
    col_devs = rounds // col_blks
    x = lax.axis_index('row')
    sub = lax.axis_index('sub')
    c = lax.axis_index('col')
    r = x * sub_devs + sub
    other_x, other_sub, other_c = 1 - x, 1 - sub, 1 - c
    peers = [{'row': x, 'sub': other_sub}, {'row': other_x, 'sub': sub}, {'row': other_x, 'sub': other_sub},
             {'col': other_c}]

    loads = [pltpu.make_async_copy(x_hbm.at[:, :, j * blk:(j + 1) * blk], cur.at[j], in_sem.at[j])
             for j in range(col_blks)]
    for load in loads:
        load.start()
    barrier = pltpu.get_barrier_semaphore()
    for peer in peers:
        pl.semaphore_signal(barrier, inc=1, device_id=peer, device_id_type=MESH)
    pl.semaphore_wait(barrier, len(peers))
    for load in loads:
        load.wait()

    def to_sibling(n, lo, count, recv):
        part = row_pan.at[n, :, pl.ds(lo, count), :]
        return pltpu.make_async_remote_copy(part, part, row_send.at[n, 0], row_recv.at[n, recv],
                                            device_id={'sub': other_sub}, device_id_type=MESH)

    def to_chip(n, lo, count, sub_to):
        part = row_pan.at[n, :, pl.ds(lo, count), :]
        return pltpu.make_async_remote_copy(part, part, row_send.at[n, 1], row_recv.at[n, 0],
                                            device_id={'row': other_x, 'sub': sub_to}, device_id_type=MESH)

    def relay(n, lo):
        part = row_pan.at[n, :, pl.ds(lo, half), :]
        return pltpu.make_async_remote_copy(part, part, relay_send.at[n], row_recv.at[n, 1],
                                            device_id={'sub': other_sub}, device_id_type=MESH)

    def col_copy(n, b):
        part = col_pan.at[n, b]
        return pltpu.make_async_remote_copy(part, part, col_send.at[n], col_recv.at[n, b],
                                            device_id={'col': other_c}, device_id_type=MESH)

    def diag_copy(n):
        return pltpu.make_async_remote_copy(diag.at[n], diag.at[n], diag_send.at[n], diag_recv.at[n],
                                            device_id={'col': other_c}, device_id_type=MESH)

    def out_copies(b):
        return [pltpu.make_async_copy(cur.at[j, b], o_hbm.at[b, :, j * blk:(j + 1) * blk],
                                      out_sem.at[b, j])
                for j in range(col_blks)]

    def one_round(step, carry):
        k = step - 1
        nxt = step
        has_main = step > 0
        has_next = step < rounds
        own_k = (step + row_devs - 1) % row_devs
        own_n = step % row_devs
        is_owner = has_main & (r == own_k)
        is_next = has_next & (r == own_n)
        col_owner = has_main & (c == (step + col_devs - 1) % col_devs)
        col_next = has_next & (c == step % col_devs)
        first = ((step - r + 2 + row_devs) // row_devs + row_blks - 1) % row_blks
        k_c = lax.max(k, 0)
        n_c = lax.min(nxt, rounds - 1)
        q = n_c // col_devs
        far_k = x != own_k // sub_devs
        far_n = has_next & (x != own_n // sub_devs)
        my_lo = sub * half
        other_lo = other_sub * half

        @pl.when(has_main & far_k)
        def _():
            pltpu.make_async_remote_copy(
                row_pan.at[k_c, :, pl.ds(other_lo, half), :], row_pan.at[k_c, :, pl.ds(other_lo, half), :],
                relay_send.at[k_c], row_recv.at[k_c, 1], device_id={'sub': other_sub}, device_id_type=MESH).wait_recv()

        @pl.when(has_main & jnp.logical_not(far_k) & jnp.logical_not(is_owner))
        def _():
            to_sibling(k_c, 0, blk, 0).wait_recv()

        def one_chunk(t, carry):
            i = t // chunks
            ch = t % chunks
            b = (first + i) % row_blks
            lo = pl.multiple_of(ch * CHUNK, CHUNK)
            active = has_main & jnp.logical_not(is_owner & (i == 0))

            @pl.when(active & (ch == 0) & jnp.logical_not(col_owner))
            def _():
                col_copy(k_c, b).wait_recv()

            @pl.when(active)
            def _():
                mine = cur.at[:, b, pl.ds(lo, CHUNK), :]
                min_plus_rows(col_pan.at[k_c, b, pl.ds(lo, CHUNK), :], row_pan.at[k_c], mine, mine)

            @pl.when((ch == chunks - 1) & col_next)
            def _():
                col_pan[n_c, b] = cur[q, b]

                @pl.when(jnp.logical_not(is_next & (i == 0)))
                def _():
                    col_copy(n_c, b).start()

            @pl.when((ch == chunks - 1) & (step == rounds))
            def _():
                for copy in out_copies(b):
                    copy.start()

            @pl.when((t == chunks - 1) & is_next & col_next)
            def _():
                close_block(col_pan.at[n_c, b], diag.at[n_c], spread)
                diag_copy(n_c).start()

            @pl.when((t == 2 * chunks - 1) & is_next)
            def _():
                @pl.when(jnp.logical_not(col_next))
                def _():
                    diag_copy(n_c).wait_recv()

                def panel_chunk(h, carry):
                    at = pl.multiple_of(h * CHUNK, CHUNK)
                    min_plus_rows(diag.at[n_c, pl.ds(at, CHUNK), :], cur.at[:, first],
                                  cur.at[:, first, pl.ds(at, CHUNK), :], row_pan.at[n_c, :, pl.ds(at, CHUNK), :])
                    to_sibling(n_c, at, CHUNK, 0).start()
                    to_chip(n_c, at, CHUNK, at // half).start()
                    return carry
                lax.fori_loop(0, chunks, panel_chunk, 0)
                cur[:, first] = row_pan[n_c]

            @pl.when((t == (row_blks - 1) * chunks + chunks // 2 - 1) & far_n)
            def _():
                to_chip(n_c, my_lo, half, sub).wait_recv()
                relay(n_c, my_lo).start()
            return carry

        lax.fori_loop(0, row_blks * chunks, one_chunk, 0)

        @pl.when(is_owner)
        def _():
            to_sibling(k_c, 0, blk, 0).wait_send()
            to_chip(k_c, 0, blk, 0).wait_send()

        @pl.when(is_owner & col_owner)
        def _():
            diag_copy(k_c).wait_send()

        @pl.when(has_main & far_k)
        def _():
            relay(k_c, my_lo).wait_send()

        @pl.when(col_owner)
        def _():
            for i in range(row_blks):
                @pl.when(jnp.logical_not(is_owner & (first == i)))
                def _():
                    col_copy(k_c, i).wait_send()
        return carry

    lax.fori_loop(0, rounds + 1, one_round, 0)
    for b in range(row_blks):
        for copy in out_copies(b):
            copy.wait()


def solution(mesh):
    sub_devs = mesh.shape['sub']
    row_devs = mesh.shape['row'] * sub_devs
    col_devs = mesh.shape['col']
    dist_spec = P(('parts', 'row', 'sub'), None, 'col')

    def local_run(local_dist):
        row_blks, blk, cols_width = local_dist.shape
        col_blks = cols_width // blk
        rounds = row_blks * row_devs
        dma = pltpu.SemaphoreType.DMA
        return pl.pallas_call(
            functools.partial(kernel, rounds, row_devs, sub_devs),
            out_shape=jax.ShapeDtypeStruct(local_dist.shape, local_dist.dtype),
            in_specs=[pl.BlockSpec(memory_space=pl.ANY)],
            out_specs=pl.BlockSpec(memory_space=pl.ANY),
            scratch_shapes=[
                pltpu.VMEM((col_blks, row_blks, blk, blk), jnp.float32),
                pltpu.VMEM((rounds, col_blks, blk, blk), jnp.float32),
                pltpu.VMEM((rounds, row_blks, blk, blk), jnp.float32),
                pltpu.VMEM((rounds, blk, blk), jnp.float32),
                pltpu.VMEM((GROUP + 1, GROUP, blk), jnp.float32),
                dma((col_blks,)), dma((row_blks, col_blks)),
                dma((rounds, 2)), dma((rounds, 2)), dma((rounds,)),
                dma((rounds,)), dma((rounds, row_blks)),
                dma((rounds,)), dma((rounds,)),
            ],
            compiler_params=pltpu.CompilerParams(
                collective_id=0, has_side_effects=True, vmem_limit_bytes=40 * 1024 * 1024),
            name='apsp',
        )(local_dist)

    return jax.shard_map(local_run, mesh=mesh, in_specs=(dist_spec,), out_specs=dist_spec, check_vma=False)
```

time: 3600 us -> 399 us (0.11)
  other arithmetic: 1990 us -> 0 us
  waiting for transfers between devices: 1100 us -> 0 us
  local copies, waits for them, and re-layouts: 410 us -> 2.91 us
  Pallas kernels: 0 us -> 396 us
  loops' own time: 71.1 us -> 0 us
    reduce_min x48 -> x0, other arithmetic: 1780 us -> none  [min_plus(): jnp.min(jnp.expand_dims(left_mat, -1) + jnp.expand_dims(right_mat, -3), a...]
    pmin x48 -> x0, waiting for transfers between devices: 1090 us -> none  [the longest x16 647 us: local_run(): lax.pmin(jnp.where(in_row & in_col, diag_blk, jnp.inf), ('row', 'sub', 'c...]
    pallas_call x0 -> x1, Pallas kernels: none -> 396 us  [local_run(): pl.pallas_call(functools.partial(kernel, rounds, row_devs, sub_devs), out...]
    dynamic_slice x2048 -> x0, local copies, waits for them, and re-layouts: 354 us -> none  [pivot_step(): col_vec = lax.dynamic_slice_in_dim(current, pivot_idx, 1, axis=last_axis)]
    min x2064 -> x0, other arithmetic: 181 us -> none  [the longest x2048 168 us: pivot_step(): return jnp.minimum(current, col_vec + row_vec)]
    another operation x16 -> x0, loops' own time: 71.1 us -> none  [close_block(): return lax.fori_loop(0, block_in.shape[-1], pivot_step, block_in)]
    add x2064 -> x0, local copies, waits for them, and re-layouts: 39 us -> none  [the longest x2048 24.8 us: pivot_step(): return jnp.minimum(current, col_vec + row_vec)]
where the time goes in v1:
time: 399 us
  Pallas kernels  396 us (99%)
    pallas_call x1, Pallas kernels, local_run(): pl.pallas_call(functools.partial(kernel, rounds, row_devs, sub_devs), out...  396 us

profile of v1, /device:TPU:7, one launch (start us, length us, event | category | flops | bytes accessed | tf_op | source)
XLA Modules:
  0.0 399.2 jit_solution(18396284182832487351)
XLA Ops:
  0.0 0.0 copy-start
  0.0 1.6 copy-done
  1.6 396.3 %apsp.1 = f32[4,128,1024]{2,1,0:T(8,128)S(1)} custom-call(f32[4,128,1024]{2,1,0:T(8,128)S(1)} %copy-done), custom_call_target="tpu_custom_call" | custom-call | tf_op jit(solution)/shard_map/apsp/pallas_call | solution.py:232
  397.9 1.3 copy.3
Async XLA Ops:
  0.0 1.6 copy-start

commit v2 on v1

--- a/solution.py
+++ b/solution.py
@@ -10,6 +10,7 @@
 MESH = pl.DeviceIdType.MESH
 CHUNK = 16
 GROUP = 8
+PANEL_AT = 3
 
 
 def close_block(src, dst, spread):
@@ -133,23 +134,27 @@
         def _():
             to_sibling(k_c, 0, blk, 0).wait_recv()
 
-        def one_chunk(t, carry):
-            i = t // chunks
-            ch = t % chunks
-            b = (first + i) % row_blks
-            lo = pl.multiple_of(ch * CHUNK, CHUNK)
-            active = has_main & jnp.logical_not(is_owner & (i == 0))
-
-            @pl.when(active & (ch == 0) & jnp.logical_not(col_owner))
-            def _():
-                col_copy(k_c, b).wait_recv()
-
-            @pl.when(active)
-            def _():
+        def update(b, lo_chunk, count):
+            def one_chunk(h, carry):
+                lo = pl.multiple_of((lo_chunk + h) * CHUNK, CHUNK)
                 mine = cur.at[:, b, pl.ds(lo, CHUNK), :]
                 min_plus_rows(col_pan.at[k_c, b, pl.ds(lo, CHUNK), :], row_pan.at[k_c], mine, mine)
-
-            @pl.when((ch == chunks - 1) & col_next)
+                return carry
+            lax.fori_loop(0, count, one_chunk, 0)
+
+        def one_half(t, carry):
+            i = t // 2
+            h = t % 2
+            b = (first + i) % row_blks
+            active = has_main & jnp.logical_not(is_owner & (i == 0))
+
+            @pl.when(active & (h == 0) & jnp.logical_not(col_owner))
+            def _():
+                col_copy(k_c, b).wait_recv()
+
+            update(b, h * (chunks // 2), jnp.where(active, chunks // 2, 0))
+
+            @pl.when((h == 1) & col_next)
             def _():
                 col_pan[n_c, b] = cur[q, b]
 
@@ -157,17 +162,17 @@
                 def _():
                     col_copy(n_c, b).start()
 
-            @pl.when((ch == chunks - 1) & (step == rounds))
+            @pl.when((h == 1) & (step == rounds))
             def _():
                 for copy in out_copies(b):
                     copy.start()
 
-            @pl.when((t == chunks - 1) & is_next & col_next)
+            @pl.when((t == 1) & is_next & col_next)
             def _():
                 close_block(col_pan.at[n_c, b], diag.at[n_c], spread)
                 diag_copy(n_c).start()
 
-            @pl.when((t == 2 * chunks - 1) & is_next)
+            @pl.when(is_next & (t == jnp.where(col_next, 1, PANEL_AT)))
             def _():
                 @pl.when(jnp.logical_not(col_next))
                 def _():
@@ -183,13 +188,13 @@
                 lax.fori_loop(0, chunks, panel_chunk, 0)
                 cur[:, first] = row_pan[n_c]
 
-            @pl.when((t == (row_blks - 1) * chunks + chunks // 2 - 1) & far_n)
+            @pl.when((t == 2 * row_blks - 2) & far_n)
             def _():
                 to_chip(n_c, my_lo, half, sub).wait_recv()
                 relay(n_c, my_lo).start()
             return carry
 
-        lax.fori_loop(0, row_blks * chunks, one_chunk, 0)
+        lax.fori_loop(0, 2 * row_blks, one_half, 0)
 
         @pl.when(is_owner)
         def _():

time: 399 us -> 369 us (0.925)
  Pallas kernels: 396 us -> 366 us
    pallas_call x1, Pallas kernels: 396 us -> 366 us  [local_run(): pl.pallas_call(functools.partial(kernel, rounds, row_devs, sub_devs), out...]
where the time goes in v2:
time: 369 us
  Pallas kernels  366 us (99%)
    pallas_call x1, Pallas kernels, local_run(): pl.pallas_call(functools.partial(kernel, rounds, row_devs, sub_devs), out...  366 us

profile of v2, /device:TPU:7, one launch (start us, length us, event | category | flops | bytes accessed | tf_op | source)
XLA Modules:
  0.0 369.0 jit_solution(11449776867859653582)
XLA Ops:
  0.0 0.0 copy-start
  0.0 1.6 copy-done
  1.6 366.0 %apsp.1 = f32[4,128,1024]{2,1,0:T(8,128)S(1)} custom-call(f32[4,128,1024]{2,1,0:T(8,128)S(1)} %copy-done), custom_call_target="tpu_custom_call" | custom-call | tf_op jit(solution)/shard_map/apsp/pallas_call | solution.py:237
  367.6 1.3 copy.3
Async XLA Ops:
  0.0 1.6 copy-start

commit v3 on v2

--- a/solution.py
+++ b/solution.py
@@ -8,7 +8,12 @@
 from jax.sharding import PartitionSpec as P
 
 MESH = pl.DeviceIdType.MESH
-CHUNK = 16
+CHUNK = 64
+PANEL_CHUNK = 16
+PART = 16
+AHEAD = 104
+PAD = 8
+RELAY_AT = 6
 GROUP = 8
 PANEL_AT = 3
 
@@ -17,10 +22,10 @@
     size = src.shape[0]
     tiles_n = size // GROUP
     tile_of = lambda x: jnp.broadcast_to(x, (GROUP, size))
+    column_of = lambda tile, g, b: tile_of(tile[:, GROUP * g + b:GROUP * g + b + 1])
     tiles = [src[GROUP * i:GROUP * (i + 1), :] for i in range(tiles_n)]
     for g in range(tiles_n):
-        column = lambda i, b: tile_of(tiles[i][:, GROUP * g + b:GROUP * g + b + 1])
-        own = [column(g, b) for b in range(GROUP)]
+        own = [column_of(tiles[g], g, b) for b in range(GROUP)]
         for b in range(GROUP):
             spread[b] = own[b]
         spread[GROUP] = tiles[g]
@@ -34,25 +39,36 @@
                 for b in range(m + 1, GROUP):
                     if a != b:
                         entry[a][b] = jnp.minimum(entry[a][b], entry[a][m] + entry[m][b])
-        for i in [(g + 1 + n) % tiles_n for n in range(tiles_n)]:
-            cols = own if i == g else [column(i, b) for b in range(GROUP)]
+        before = list(tiles)
+        following = (g + 1) % tiles_n
+        others = [(g + 2 + n) % tiles_n for n in range(tiles_n - 1)]
+        for part in ([following], others):
             for b in range(GROUP):
-                tiles[i] = jnp.minimum(tiles[i], cols[b] + rows[b])
+                for i in part:
+                    column = own[b] if i == g else column_of(before[i], g, b)
+                    tiles[i] = jnp.minimum(tiles[i], column + rows[b])
     for i in range(tiles_n):
         dst[GROUP * i:GROUP * (i + 1), :] = tiles[i]
 
 
 def min_plus_rows(left, right, init, out):
-    left_rows = left[...]
-    acc = init[...]
-    for l in range(left.shape[1]):
-        acc = jnp.minimum(acc, left_rows[:, l:l + 1][None] + right[:, l:l + 1, :])
-    out[...] = acc
+    parts = left.shape[0] // PART
+    left_rows = left[0:PART, :]
+    for u in range(parts):
+        acc = init[:, u * PART:(u + 1) * PART, :]
+        for l in range(left.shape[1]):
+            acc = jnp.minimum(acc, left_rows[:, l:l + 1][None] + right[:, l:l + 1, :])
+            if l == AHEAD and u + 1 < parts:
+                ahead = left[(u + 1) * PART:(u + 2) * PART, :]
+                ahead = jnp.minimum(ahead, jnp.maximum(ahead, acc[0]))
+        out[:, u * PART:(u + 1) * PART, :] = acc
+        left_rows = ahead if u + 1 < parts else None
 
 
 def kernel(rounds, row_devs, sub_devs, x_hbm, o_hbm, cur, row_pan, col_pan, diag, spread,
            in_sem, out_sem, row_send, row_recv, relay_send, col_send, col_recv, diag_send, diag_recv):
-    col_blks, row_blks, blk, _ = cur.shape
+    row_blks, blk = col_pan.shape[1:3]
+    col_blks = cur.shape[0]
     chunks = blk // CHUNK
     half = blk // sub_devs
     col_devs = rounds // col_blks
@@ -64,8 +80,11 @@
     peers = [{'row': x, 'sub': other_sub}, {'row': other_x, 'sub': sub}, {'row': other_x, 'sub': other_sub},
              {'col': other_c}]
 
-    loads = [pltpu.make_async_copy(x_hbm.at[:, :, j * blk:(j + 1) * blk], cur.at[j], in_sem.at[j])
-             for j in range(col_blks)]
+    def block(b, lo, count):
+        return pl.ds(pl.multiple_of(b * blk + lo, PANEL_CHUNK), count)
+
+    loads = [pltpu.make_async_copy(x_hbm.at[b, :, j * blk:(j + 1) * blk], cur.at[j, block(b, 0, blk)], in_sem.at[b, j])
+             for b in range(row_blks) for j in range(col_blks)]
     for load in loads:
         load.start()
     barrier = pltpu.get_barrier_semaphore()
@@ -100,7 +119,7 @@
                                             device_id={'col': other_c}, device_id_type=MESH)
 
     def out_copies(b):
-        return [pltpu.make_async_copy(cur.at[j, b], o_hbm.at[b, :, j * blk:(j + 1) * blk],
+        return [pltpu.make_async_copy(cur.at[j, block(b, 0, blk)], o_hbm.at[b, :, j * blk:(j + 1) * blk],
                                       out_sem.at[b, j])
                 for j in range(col_blks)]
 
@@ -137,8 +156,8 @@
         def update(b, lo_chunk, count):
             def one_chunk(h, carry):
                 lo = pl.multiple_of((lo_chunk + h) * CHUNK, CHUNK)
-                mine = cur.at[:, b, pl.ds(lo, CHUNK), :]
-                min_plus_rows(col_pan.at[k_c, b, pl.ds(lo, CHUNK), :], row_pan.at[k_c], mine, mine)
+                mine = cur.at[:, block(b, lo, CHUNK), :]
+                min_plus_rows(col_pan.at[k_c, b, pl.ds(lo, CHUNK), :], row_pan.at[k_c, :, 0:blk, :], mine, mine)
                 return carry
             lax.fori_loop(0, count, one_chunk, 0)
 
@@ -156,7 +175,7 @@
 
             @pl.when((h == 1) & col_next)
             def _():
-                col_pan[n_c, b] = cur[q, b]
+                col_pan[n_c, b] = cur[q, block(b, 0, blk), :]
 
                 @pl.when(jnp.logical_not(is_next & (i == 0)))
                 def _():
@@ -179,16 +198,17 @@
                     diag_copy(n_c).wait_recv()
 
                 def panel_chunk(h, carry):
-                    at = pl.multiple_of(h * CHUNK, CHUNK)
-                    min_plus_rows(diag.at[n_c, pl.ds(at, CHUNK), :], cur.at[:, first],
-                                  cur.at[:, first, pl.ds(at, CHUNK), :], row_pan.at[n_c, :, pl.ds(at, CHUNK), :])
-                    to_sibling(n_c, at, CHUNK, 0).start()
-                    to_chip(n_c, at, CHUNK, at // half).start()
+                    at = pl.multiple_of(h * PANEL_CHUNK, PANEL_CHUNK)
+                    min_plus_rows(diag.at[n_c, pl.ds(at, PANEL_CHUNK), :], cur.at[:, block(first, 0, blk), :],
+                                  cur.at[:, block(first, at, PANEL_CHUNK), :],
+                                  row_pan.at[n_c, :, pl.ds(at, PANEL_CHUNK), :])
+                    to_sibling(n_c, at, PANEL_CHUNK, 0).start()
+                    to_chip(n_c, at, PANEL_CHUNK, at // half).start()
                     return carry
-                lax.fori_loop(0, chunks, panel_chunk, 0)
-                cur[:, first] = row_pan[n_c]
-
-            @pl.when((t == 2 * row_blks - 2) & far_n)
+                lax.fori_loop(0, blk // PANEL_CHUNK, panel_chunk, 0)
+                cur[:, block(first, 0, blk), :] = row_pan[n_c, :, 0:blk, :]
+
+            @pl.when((t == RELAY_AT) & far_n)
             def _():
                 to_chip(n_c, my_lo, half, sub).wait_recv()
                 relay(n_c, my_lo).start()
@@ -240,12 +260,12 @@
             in_specs=[pl.BlockSpec(memory_space=pl.ANY)],
             out_specs=pl.BlockSpec(memory_space=pl.ANY),
             scratch_shapes=[
-                pltpu.VMEM((col_blks, row_blks, blk, blk), jnp.float32),
-                pltpu.VMEM((rounds, col_blks, blk, blk), jnp.float32),
+                pltpu.VMEM((col_blks, row_blks * blk + PAD, blk), jnp.float32),
+                pltpu.VMEM((rounds, col_blks, blk + PAD, blk), jnp.float32),
                 pltpu.VMEM((rounds, row_blks, blk, blk), jnp.float32),
                 pltpu.VMEM((rounds, blk, blk), jnp.float32),
                 pltpu.VMEM((GROUP + 1, GROUP, blk), jnp.float32),
-                dma((col_blks,)), dma((row_blks, col_blks)),
+                dma((row_blks, col_blks)), dma((row_blks, col_blks)),
                 dma((rounds, 2)), dma((rounds, 2)), dma((rounds,)),
                 dma((rounds,)), dma((rounds, row_blks)),
                 dma((rounds,)), dma((rounds,)),

time: 369 us -> 363 us (0.984)
  Pallas kernels: 366 us -> 359 us
    pallas_call x1, Pallas kernels: 366 us -> 359 us  [local_run(): pl.pallas_call(functools.partial(kernel, rounds, row_devs, sub_devs), out...]
where the time goes in v3:
time: 363 us; the launch traced here: 362 us
  Pallas kernels  359 us (99%)
    pallas_call x1, Pallas kernels, local_run(): pl.pallas_call(functools.partial(kernel, rounds, row_devs, sub_devs), out...  359 us

profile of v3, /device:TPU:7, one launch (start us, length us, event | category | flops | bytes accessed | tf_op | source)
XLA Modules:
  0.0 362.4 jit_solution(11561794920351594112)
XLA Ops:
  0.0 0.0 copy-start
  0.0 1.6 copy-done
  1.6 359.5 %apsp.1 = f32[4,128,1024]{2,1,0:T(8,128)S(1)} custom-call(f32[4,128,1024]{2,1,0:T(8,128)S(1)} %copy-done), custom_call_target="tpu_custom_call" | custom-call | tf_op jit(solution)/shard_map/apsp/pallas_call | solution.py:257
  361.1 1.3 copy.3
Async XLA Ops:
  0.0 1.6 copy-start
